TPU v7x, 32 devices: a whole 2x2x4 slice. The times are simulated.
32 devices in a mesh: expert: 8 (over z, core), row: 4 (over y, x).
Axes of the slice: x: 2, y: 2, z: 4, core: 2. Of those that a mesh axis runs over, the one named last changes fastest.
Arguments:
- grads: bfloat16 [8, 7168, 2048], P('expert', 'row')
- basis: bfloat16 [8, 7168, 256], P('expert', 'row'), may hold values from -0.0625 to 0.0625
- loads: int32 [8], P('expert'), may hold values from 1 to 1, as said below
- flags: int32 [8], P('expert'), may hold values 0 or 1
Outputs:
- new_basis: float32 [8, 7168, 256], P('expert', 'row')
- rotated: float32 [8, 256, 2048], P('expert', None, 'row')
Inputs may be any that keep to these rules, and one draw needn't show every extreme that they name: Slots 0 to loads[d] - 1 of expert-axis index d are live and hold experts; the others are empty. Some index has all 1 slots live.
All inputs are finite; a program needn't handle non-finite values. No bound on the sum of `flags` on one device may be relied on, other than what follows from the above.
Results may differ from a plain program's by a relative error of at most 0.006.
Values sent between devices are 32-bit elements; how exact they have to be, the bound alone decides.
A program may use at most 64 MiB of HBM per device.

v0:
```python
import jax
import jax.numpy as jnp
from jax import lax
from jax.sharding import PartitionSpec as P

D = 7168
S = 2048


def on_device(grads, basis, loads, flags):
    slot_count = grads.shape[0]
    live_count = loads[0]
    live_mask = jnp.arange(slot_count, dtype=jnp.int32) < live_count
    refresh = jnp.logical_and(live_mask, flags == 1)
    live_cube = live_mask[:, None, None]
    refresh_cube = refresh[:, None, None]
    squares = jnp.sum(jnp.where(live_cube, jnp.square(grads.astype(jnp.float32)), 0.0))
    leader = (lax.axis_index("row") == 0).astype(jnp.float32)
    total_sq, total_live = lax.psum(
        (squares, leader * live_count.astype(jnp.float32)), ("expert", "row")
    )
    norm_scale = lax.rsqrt(total_sq / (total_live * D * S) + 1e-06)
    local_inner = jnp.einsum("cds,cdk->csk", grads, basis, preferred_element_type=jnp.float32)
    inner_sum = jnp.stack([lax.psum(local_inner[0], "row")])
    inner_gram = jnp.einsum("csk,csj->ckj", inner_sum, inner_sum, precision=lax.Precision.HIGHEST)
    inner_half = inner_sum.astype(jnp.bfloat16)
    power_rows = jnp.einsum(
        "cds,csk->cdk", grads, inner_half, preferred_element_type=jnp.float32
    ).astype(jnp.bfloat16)
    projector = jnp.where(refresh_cube, power_rows, basis)
    local_cross = jnp.einsum("cdk,cds->cks", projector, grads, preferred_element_type=jnp.float32)
    identity = jnp.eye(basis.shape[2], dtype=jnp.float32)
    lower_first = jnp.linalg.cholesky(jnp.where(refresh_cube, inner_gram, identity))
    first_rows = lax.linalg.triangular_solve(
        lower_first, power_rows.astype(jnp.float32), left_side=False, lower=True, transpose_a=True
    )
    local_second = jnp.einsum(
        "cdk,cdj->ckj", first_rows, first_rows, precision=lax.Precision.HIGHEST
    )
    gram_again = lax.psum(local_second, "row")
    cross_cols = lax.psum_scatter(local_cross, "row", scatter_dimension=2, tiled=True)
    lower_second = jnp.linalg.cholesky(jnp.where(refresh_cube, gram_again, identity))
    fresh_basis = lax.linalg.triangular_solve(
        lower_second, first_rows, left_side=False, lower=True, transpose_a=True
    )
    half_solved = lax.linalg.triangular_solve(lower_first, cross_cols, left_side=True, lower=True)
    fresh_rot = lax.linalg.triangular_solve(lower_second, half_solved, left_side=True, lower=True)
    new_basis = jnp.where(
        refresh_cube, fresh_basis, jnp.where(live_cube, basis.astype(jnp.float32), 0.0)
    )
    rotated = jnp.where(refresh_cube, fresh_rot, jnp.where(live_cube, cross_cols, 0.0)) * norm_scale
    return (new_basis, rotated)


def solution(mesh):
    placed = (P("expert", "row", None), P("expert", "row", None), P("expert"), P("expert"))
    return jax.shard_map(
        on_device,
        mesh=mesh,
        in_specs=placed,
        out_specs=(P("expert", "row", None), P("expert", None, "row")),
        check_vma=False,
    )
```

profile of v0, /device:TPU:0, one launch (start us, length us, event | category | flops | bytes accessed | tf_op | source)
XLA Modules:
  0.0 307.3 jit_solution(6141670956639925859)
XLA Ops:
  7.2 6.8 %fusion.4 = f32[2048,256]{1,0:T(8,128)} fusion(bf16[1,1792,2048]{2,1,0:T(8,128)(2,1)} %param.9, bf16[1,1792,256]{2,1,0:T(8,128)(2,1)} %param.10), kind=kOutput, calls=%fused_computation.9 | convolution fusion | flops 1879048192 | bytes 10354688 | tf_op jit(solution)/shard_map/cds,cdk->csk/dot_general | solution.py:23
  14.1 1.1 copy-done.2
  15.2 1.1 copy.12
  17.7 68.7 %all-reduce.5.cloned.1.call-done = f32[2048,256]{1,0:T(8,128)} async-done(((f32[2048,256]{1,0:T(8,128)}), f32[2048,256]{1,0:T(8,128)}) %all-reduce.5.cloned.1.call-update) | async-done | bytes 2097168 | tf_op jit(solution)/shard_map/psum | solution.py:24
  86.4 5.7 %convolution_select_fusion = f32[256,256]{0,1:T(8,128)S(1)} fusion(f32[2048,256]{1,0:T(8,128)} %all-reduce.5.cloned.1.call-done, pred[]{:T(512)} %bitcast), kind=kOutput, calls=%fused_computation.32 | convolution fusion | flops 1610809344 | bytes 2359297 | tf_op jit(solution)/shard_map/csk,csj->ckj/dot_general | solution.py:25
  93.0 11.7 %custom-call.21 = f32[1,128,128]{2,1,0:T(8,128)S(1)} custom-call(f32[1,128,128]{2,1,0:T(8,128)S(1)} %cholesky.191), custom_call_target="Cholesky" | custom-call | tf_op jit(solution)/shard_map/jit(cholesky)/cholesky | solution.py:33
  104.7 9.8 %custom-call.22 = f32[1,1,128,128]{2,3,1,0:T(8,128)S(1)} custom-call(f32[1,1,128,128]{3,2,1,0:T(8,128)S(1)} %get-tuple-element.68), custom_call_target="InvertDiagBlocksLowerTriangular" | custom-call | tf_op jit(solution)/shard_map/jit(cholesky)/cholesky | solution.py:33
  114.6 1.0 bitcast_dynamic-update-slice_fusion.3
  115.6 1.1 fusion.27
  116.7 11.9 %custom-call.23 = f32[1,128,128]{2,1,0:T(8,128)S(1)} custom-call(f32[1,128,128]{2,1,0:T(8,128)S(1)} %fusion.27), custom_call_target="Cholesky" | custom-call | tf_op jit(solution)/shard_map/jit(cholesky)/cholesky | solution.py:33
  130.7 3.9 %while.8 = (s32[]{:T(128)}, f32[1,256,256]{2,1,0:T(8,128)S(1)}, s32[2,2]{1,0:T(2,128)S(1)}, f32[2,1,128,128]{3,2,1,0:T(8,128)S(1)}, s32[]{:T(128)}) while((s32[]{:T(128)}, f32[1,256,256]{2,1,0:T(8,128)S(1)}, s32[2,2]{1,0:T(2,128)S(1)}, f32[2,1,128,128]{3,2,1,0:T(8,128)S(1)}, s32[]{:T(128)}) %tuple.57), condition=%wide.while_cond, body=%wide.while_body.sunk | while | flops 2 | bytes 131181 | solution.py:34
  131.3 1.4 bitcast_dynamic-update-slice_fusion.6
  133.3 1.4 bitcast_dynamic-update-slice_fusion.6
  134.6 19.7 %custom-call.24 = f32[1,2,128,128]{2,3,1,0:T(8,128)S(1)} custom-call(f32[1,2,128,128]{3,2,1,0:T(8,128)S(1)} %bitcast.221), custom_call_target="InvertDiagBlocksLowerTriangular" | custom-call | tf_op jit(solution)/shard_map/triangular_solve/custom-call.0 | solution.py:34
  154.3 6.2 %fusion.53 = (f32[1,1792,256]{1,2,0:T(8,128)S(1)}, bf16[1,1792,256]{1,2,0:T(8,128)(2,1)}) fusion(bf16[1,1792,2048]{2,1,0:T(8,128)(2,1)} %param.9, f32[2048,256]{1,0:T(8,128)S(1)} %copy-done), kind=kOutput, calls=%fused_computation.99 | convolution fusion | flops 1880489984 | bytes 12189696 | tf_op jit(solution)/shard_map/cds,csk->cdk/dot_general | solution.py:27
  163.4 2.4 fusion.22
  165.9 6.8 %fusion.6 = f32[1,256,2048]{2,1,0:T(8,128)} fusion(bf16[1,1792,2048]{2,1,0:T(8,128)(2,1)} %param.9, bf16[1,1792,256]{1,2,0:T(8,128)(2,1)} %get-tuple-element.70, bf16[1,1792,256]{1,2,0:T(8,128)(2,1)S(1)} %copy.12, pred[]{:T(512)} %bitcast), kind=kOutput, calls=%fused_computation.11 | convolution fusion | flops 1879506944 | bytes 11272193 | tf_op jit(solution)/shard_map/cdk,cds->cks/dot_general | solution.py:31
  172.7 7.5 %select_reduce_fusion = f32[]{:T(128)} fusion(bf16[1,1792,2048]{2,1,0:T(8,128)(2,1)} %param.9, pred[]{:T(512)} %bitcast.40), kind=kLoop, calls=%fused_computation.4 | loop fusion | flops 14680063 | bytes 7340037 | tf_op jit(solution)/shard_map/reduce_sum | solution.py:17
  180.2 39.4 %all-reduce.1 = (f32[]{:T(128)}, f32[]{:T(128)}) all-reduce(f32[]{:T(128)} %select_reduce_fusion, f32[]{:T(128)S(6)} %mul.13), channel_id=1, replica_groups=mesh['expert'=8,'row'=4] {'expert','row'}, use_global_device_ids=true, to_apply=%region_8.12 | all-reduce | flops 2 | bytes 16 | tf_op jit(solution)/shard_map/psum | solution.py:19
  222.1 1.0 fusion.40
  223.1 12.3 %custom-call.25 = f32[1,128,128]{2,1,0:T(8,128)} custom-call(f32[1,128,128]{2,1,0:T(8,128)S(1)} %cholesky.194), custom_call_target="Cholesky" | custom-call | tf_op jit(solution)/shard_map/jit(cholesky)/cholesky | solution.py:42
  236.3 1.5 select_reduce_fusion.2
  237.8 11.3 %custom-call.26 = f32[1,1,128,128]{2,3,1,0:T(8,128)} custom-call(f32[1,1,128,128]{3,2,1,0:T(8,128)} %get-tuple-element.64), custom_call_target="InvertDiagBlocksLowerTriangular" | custom-call | tf_op jit(solution)/shard_map/jit(cholesky)/cholesky | solution.py:42
  249.1 1.0 bitcast_dynamic-update-slice_fusion.2
  251.1 12.5 %custom-call.27 = f32[1,128,128]{2,1,0:T(8,128)S(1)} custom-call(f32[1,128,128]{2,1,0:T(8,128)} %fusion.28), custom_call_target="Cholesky" | custom-call | tf_op jit(solution)/shard_map/jit(cholesky)/cholesky | solution.py:42
  266.3 4.0 %while.9 = (s32[]{:T(128)}, f32[1,256,256]{2,1,0:T(8,128)S(1)}, s32[2,2]{1,0:T(2,128)S(1)}, f32[2,1,128,128]{3,2,1,0:T(8,128)S(1)}, s32[]{:T(128)}) while((s32[]{:T(128)}, f32[1,256,256]{2,1,0:T(8,128)S(1)}, s32[2,2]{1,0:T(2,128)S(1)}, f32[2,1,128,128]{3,2,1,0:T(8,128)S(1)}, s32[]{:T(128)}) %tuple.69), condition=%wide.while_cond.clone, body=%wide.while_body.clone.sunk | while | flops 2 | bytes 131181 | solution.py:43
  266.9 1.4 bitcast_dynamic-update-slice_fusion.7
  268.9 1.4 bitcast_dynamic-update-slice_fusion.7
  270.3 19.9 %custom-call.28 = f32[1,2,128,128]{2,3,1,0:T(8,128)S(1)} custom-call(f32[1,2,128,128]{3,2,1,0:T(8,128)S(1)} %bitcast.220), custom_call_target="InvertDiagBlocksLowerTriangular" | custom-call | tf_op jit(solution)/shard_map/triangular_solve/custom-call.0 | solution.py:43
  293.3 1.7 copy.14
  295.0 1.4 fusion.38
  297.3 1.3 fusion.24
  (60 shorter events, 17.0 us)
Async XLA Ops:
  7.2 79.2 %all-reduce.5.cloned.1.call-start = ((), (), s32[]{:S(2)}) async-start(), calls=%async_computation.1 | async-start | bytes 4194304 | tf_op jit(solution)/shard_map/psum | solution.py:24
  14.0 1.2 copy-start.2
  14.1 206.9 %all-reduce.7.cloned.1.call-start = ((), (), s32[]{:S(2)}) async-start(), calls=%async_computation.2 | async-start | bytes 524288 | tf_op jit(solution)/shard_map/psum | solution.py:40
  92.1 62.3 %copy-start = (f32[2048,256]{1,0:T(8,128)S(1)}, f32[2048,256]{1,0:T(8,128)}, u32[]{:S(2)}) copy-start(f32[2048,256]{1,0:T(8,128)} %all-reduce.5.cloned.1.call-done) | copy-start | bytes 6291460
  92.3 0.7 copy-start.3
  154.3 8.1 %copy-start.4 = (f32[1,2,128,128]{2,3,1,0:T(8,128)}, f32[1,2,128,128]{2,3,1,0:T(8,128)S(1)}, u32[]{:S(2)}) copy-start(f32[1,2,128,128]{2,3,1,0:T(8,128)S(1)} %custom-call.24) | copy-start | bytes 393220
  165.8 129.2 %reduce-scatter.2.cloned.1.call-start = ((), (), s32[]{:S(2)}) async-start(), calls=%async_computation.3 | async-start | bytes 2621440 | tf_op jit(solution)/shard_map/reduce_scatter | solution.py:41
  293.3 1.7 copy-start.5
  295.0 4.4 %copy-start.1 = (f32[1,256,512]{2,1,0:T(8,128)S(1)}, f32[1,256,512]{2,1,0:T(8,128)}, u32[]{:S(2)}) copy-start(f32[1,256,512]{2,1,0:T(8,128)} %reduce-scatter.2.cloned.1.call-done) | copy-start | bytes 1572868
Sparse Core Ops, SparseCore 0:
  14.2 72.1 all-reduce.4
  165.9 43.0 all-reduce.6
  211.9 35.2 reduce-scatter.1
where the time goes:
time: 311 us; the launch traced here: 307 us
  other arithmetic  123 us (40%)
  waiting for transfers between devices  68.8 us (22%)
  matrix products  42 us (14%)
  blocking collectives  39.4 us (13%)
  between operations  19.7 us (6%)
  local copies, waits for them, and re-layouts  13.7 us (4%)
    psum x1, waiting for transfers between devices, on_device(): inner_sum = jnp.stack([lax.psum(local_inner[0], 'row')])  68.7 us
    psum x1, blocking collectives, on_device(): lax.psum((squares, leader * live_count.astype(jnp.float32)), ('expert', '...  39.4 us
    another operation x7, other arithmetic, on_device(): jnp.linalg.cholesky(jnp.where(refresh_cube, gram_again, identity))  39 us
    another operation x6, other arithmetic, on_device(): jnp.linalg.cholesky(jnp.where(refresh_cube, inner_gram, identity))  34.1 us
    another operation x2, other arithmetic, on_device(): lax.linalg.triangular_solve(lower_second, first_rows, left_side=False, lo...  20 us
    another operation x3, other arithmetic, on_device(): lax.linalg.triangular_solve(lower_first, power_rows.astype(jnp.float32),...  19.7 us
    reduce_sum x1, other arithmetic, on_device(): jnp.sum(jnp.where(live_cube, jnp.square(grads.astype(jnp.float32)), 0.0))  7.48 us
    dot_general x1, matrix products, on_device(): jnp.einsum('cds,cdk->csk', grads, basis, preferred_element_type=jnp.float32)  6.82 us
  transfers between devices with their start and end apart: 3, of which 1 were waited for; matrix products, arithmetic and copies ran while one was open for 29% of the time, Pallas kernels for 0%

commit v1 on v0

--- a/solution.py
+++ b/solution.py
@@ -21,7 +21,7 @@
     )
     norm_scale = lax.rsqrt(total_sq / (total_live * D * S) + 1e-06)
     local_inner = jnp.einsum("cds,cdk->csk", grads, basis, preferred_element_type=jnp.float32)
-    inner_sum = jnp.stack([lax.psum(local_inner[0], "row")])
+    inner_sum = jnp.stack([jnp.sum(lax.all_gather(local_inner[0], "row"), axis=0)])
     inner_gram = jnp.einsum("csk,csj->ckj", inner_sum, inner_sum, precision=lax.Precision.HIGHEST)
     inner_half = inner_sum.astype(jnp.bfloat16)
     power_rows = jnp.einsum(

time: 311 us -> 332 us (1.068)
  waiting for transfers between devices: 68.8 us -> 87.2 us
  other arithmetic: 123 us -> 128 us
    all_gather x0 -> x1, waiting for transfers between devices: none -> 87.1 us  [on_device(): lax.all_gather(local_inner[0], 'row')]
    psum x1 -> x0, waiting for transfers between devices: 68.7 us -> none  [on_device(): inner_sum = jnp.stack([lax.psum(local_inner[0], 'row')])]
    reduce_sum x0 -> x1, other arithmetic: none -> 4.21 us  [on_device(): jnp.sum(lax.all_gather(local_inner[0], 'row'), axis=0)]
  transfers between devices with their start and end apart: 3 -> 3, of which waited for: 1 -> 1; matrix products, arithmetic and copies ran while one was open for 29% -> 27% of each run, Pallas kernels for 0% -> 0%
where the time goes in v1:
time: 332 us; the launch traced here: 328 us
  other arithmetic  128 us (39%)
  waiting for transfers between devices  87.2 us (26%)
  matrix products  41.3 us (12%)
  blocking collectives  39.2 us (12%)
  between operations  19.5 us (6%)
  local copies, waits for them, and re-layouts  12.8 us (4%)
    all_gather x1, waiting for transfers between devices, on_device(): lax.all_gather(local_inner[0], 'row')  87.1 us
    psum x1, blocking collectives, on_device(): lax.psum((squares, leader * live_count.astype(jnp.float32)), ('expert', '...  39.2 us
    another operation x7, other arithmetic, on_device(): jnp.linalg.cholesky(jnp.where(refresh_cube, gram_again, identity))  39 us
    another operation x6, other arithmetic, on_device(): jnp.linalg.cholesky(jnp.where(refresh_cube, inner_gram, identity))  34.4 us
    another operation x2, other arithmetic, on_device(): lax.linalg.triangular_solve(lower_second, first_rows, left_side=False, lo...  19.9 us
    another operation x3, other arithmetic, on_device(): lax.linalg.triangular_solve(lower_first, power_rows.astype(jnp.float32),...  19.7 us
    reduce_sum x1, other arithmetic, on_device(): jnp.sum(jnp.where(live_cube, jnp.square(grads.astype(jnp.float32)), 0.0))  7.49 us
    dot_general x1, matrix products, on_device(): jnp.einsum('cds,cdk->csk', grads, basis, preferred_element_type=jnp.float32)  6.97 us
  transfers between devices with their start and end apart: 3, of which 1 were waited for; matrix products, arithmetic and copies ran while one was open for 27% of the time, Pallas kernels for 0%

profile of v1, /device:TPU:0, one launch (start us, length us, event | category | flops | bytes accessed | tf_op | source)
XLA Modules:
  0.0 328.2 jit_solution(1827397809790140574)
XLA Ops:
  7.2 7.0 %fusion.4 = f32[2048,256]{1,0:T(8,128)} fusion(bf16[1,1792,2048]{2,1,0:T(8,128)(2,1)} %param.9, bf16[1,1792,256]{2,1,0:T(8,128)(2,1)} %param.10), kind=kOutput, calls=%fused_computation.9 | convolution fusion | flops 1879048192 | bytes 10354688 | tf_op jit(solution)/shard_map/cds,cdk->csk/dot_general | solution.py:23
  14.3 1.1 copy-done.1
  17.5 87.1 %all-gather.3.cloned.1.call-done = f32[8192,256]{1,0:T(8,128)} async-done(((f32[2048,256]{1,0:T(8,128)}), f32[8192,256]{1,0:T(8,128)}) %all-gather.3.cloned.1.call-update) | async-done | bytes 8388624 | tf_op jit(solution)/shard_map/all_gather | solution.py:24
  104.6 4.2 %reduce_sum.18 = f32[2048,256]{1,0:T(8,128)S(1)} reduce(f32[4,2048,256]{2,1,0:T(8,128)} %bitcast.217, f32[]{:T(128)} %constant.80.clone.1), dimensions={0}, to_apply=%region_0.1 | reduce | flops 1572864 | bytes 10485764 | tf_op jit(solution)/shard_map/reduce_sum | solution.py:24
  108.8 6.8 %fusion.53 = (f32[1,1792,256]{1,2,0:T(8,128)}, bf16[1,1792,256]{1,2,0:T(8,128)(2,1)}) fusion(bf16[1,1792,2048]{2,1,0:T(8,128)(2,1)} %param.9, f32[2048,256]{1,0:T(8,128)S(1)} %reduce_sum.18), kind=kOutput, calls=%fused_computation.99 | convolution fusion | flops 1880489984 | bytes 12189696 | tf_op jit(solution)/shard_map/cds,csk->cdk/dot_general | solution.py:27
  115.5 3.4 %convolution_select_fusion = f32[256,256]{0,1:T(8,128)S(1)} fusion(f32[2048,256]{1,0:T(8,128)S(1)} %reduce_sum.18, pred[]{:T(512)} %bitcast), kind=kOutput, calls=%fused_computation.32 | convolution fusion | flops 1610809344 | bytes 2359297 | tf_op jit(solution)/shard_map/csk,csj->ckj/dot_general | solution.py:25
  119.2 11.7 %custom-call.21 = f32[1,128,128]{2,1,0:T(8,128)S(1)} custom-call(f32[1,128,128]{2,1,0:T(8,128)S(1)} %cholesky.191), custom_call_target="Cholesky" | custom-call | tf_op jit(solution)/shard_map/jit(cholesky)/cholesky | solution.py:33
  131.0 10.2 %custom-call.22 = f32[1,1,128,128]{2,3,1,0:T(8,128)S(1)} custom-call(f32[1,1,128,128]{3,2,1,0:T(8,128)S(1)} %get-tuple-element.68), custom_call_target="InvertDiagBlocksLowerTriangular" | custom-call | tf_op jit(solution)/shard_map/jit(cholesky)/cholesky | solution.py:33
  141.6 11.7 %custom-call.23 = f32[1,128,128]{2,1,0:T(8,128)S(1)} custom-call(f32[1,128,128]{2,1,0:T(8,128)S(1)} %fusion.27), custom_call_target="Cholesky" | custom-call | tf_op jit(solution)/shard_map/jit(cholesky)/cholesky | solution.py:33
  155.5 4.1 %while.8 = (s32[]{:T(128)}, f32[1,256,256]{2,1,0:T(8,128)S(1)}, s32[2,2]{1,0:T(2,128)S(1)}, f32[2,1,128,128]{3,2,1,0:T(8,128)S(1)}, s32[]{:T(128)}) while((s32[]{:T(128)}, f32[1,256,256]{2,1,0:T(8,128)S(1)}, s32[2,2]{1,0:T(2,128)S(1)}, f32[2,1,128,128]{3,2,1,0:T(8,128)S(1)}, s32[]{:T(128)}) %tuple.57), condition=%wide.while_cond, body=%wide.while_body.sunk | while | flops 2 | bytes 131189 | solution.py:34
  156.2 1.3 bitcast_dynamic-update-slice_fusion.6
  158.2 1.3 bitcast_dynamic-update-slice_fusion.6
  159.6 19.7 %custom-call.24 = f32[1,2,128,128]{2,3,1,0:T(8,128)S(1)} custom-call(f32[1,2,128,128]{3,2,1,0:T(8,128)S(1)} %bitcast.223), custom_call_target="InvertDiagBlocksLowerTriangular" | custom-call | tf_op jit(solution)/shard_map/triangular_solve/custom-call.0 | solution.py:34
  179.3 2.2 fusion.30
  181.4 2.1 fusion.16
  184.5 2.4 fusion.22
  187.2 6.8 %fusion.6 = f32[1,256,2048]{2,1,0:T(8,128)} fusion(bf16[1,1792,2048]{2,1,0:T(8,128)(2,1)} %param.9, bf16[1,1792,256]{1,2,0:T(8,128)(2,1)} %get-tuple-element.70, bf16[1,1792,256]{1,2,0:T(8,128)(2,1)S(1)} %copy.12, pred[]{:T(512)} %bitcast), kind=kOutput, calls=%fused_computation.11 | convolution fusion | flops 1879506944 | bytes 11272193 | tf_op jit(solution)/shard_map/cdk,cds->cks/dot_general | solution.py:31
  194.0 7.5 %select_reduce_fusion = f32[]{:T(128)} fusion(bf16[1,1792,2048]{2,1,0:T(8,128)(2,1)} %param.9, pred[]{:T(512)} %bitcast.41), kind=kLoop, calls=%fused_computation.4 | loop fusion | flops 14680063 | bytes 7340037 | tf_op jit(solution)/shard_map/reduce_sum | solution.py:17
  201.5 39.2 %all-reduce.1 = (f32[]{:T(128)}, f32[]{:T(128)}) all-reduce(f32[]{:T(128)} %select_reduce_fusion, f32[]{:T(128)S(6)} %mul.13), channel_id=1, replica_groups=mesh['expert'=8,'row'=4] {'expert','row'}, use_global_device_ids=true, to_apply=%region_8.12 | all-reduce | flops 2 | bytes 16 | tf_op jit(solution)/shard_map/psum | solution.py:19
  243.2 1.0 fusion.40
  244.2 12.3 %custom-call.25 = f32[1,128,128]{2,1,0:T(8,128)} custom-call(f32[1,128,128]{2,1,0:T(8,128)S(1)} %cholesky.194), custom_call_target="Cholesky" | custom-call | tf_op jit(solution)/shard_map/jit(cholesky)/cholesky | solution.py:42
  257.4 1.5 select_reduce_fusion.2
  258.9 11.3 %custom-call.26 = f32[1,1,128,128]{2,3,1,0:T(8,128)} custom-call(f32[1,1,128,128]{3,2,1,0:T(8,128)} %get-tuple-element.64), custom_call_target="InvertDiagBlocksLowerTriangular" | custom-call | tf_op jit(solution)/shard_map/jit(cholesky)/cholesky | solution.py:42
  270.2 1.0 bitcast_dynamic-update-slice_fusion.2
  272.2 12.5 %custom-call.27 = f32[1,128,128]{2,1,0:T(8,128)S(1)} custom-call(f32[1,128,128]{2,1,0:T(8,128)} %fusion.28), custom_call_target="Cholesky" | custom-call | tf_op jit(solution)/shard_map/jit(cholesky)/cholesky | solution.py:42
  287.4 4.0 %while.9 = (s32[]{:T(128)}, f32[1,256,256]{2,1,0:T(8,128)S(1)}, s32[2,2]{1,0:T(2,128)S(1)}, f32[2,1,128,128]{3,2,1,0:T(8,128)S(1)}, s32[]{:T(128)}) while((s32[]{:T(128)}, f32[1,256,256]{2,1,0:T(8,128)S(1)}, s32[2,2]{1,0:T(2,128)S(1)}, f32[2,1,128,128]{3,2,1,0:T(8,128)S(1)}, s32[]{:T(128)}) %tuple.69), condition=%wide.while_cond.clone, body=%wide.while_body.clone.sunk | while | flops 2 | bytes 131189 | solution.py:43
  288.0 1.4 bitcast_dynamic-update-slice_fusion.7
  290.0 1.4 bitcast_dynamic-update-slice_fusion.7
  291.4 19.9 %custom-call.28 = f32[1,2,128,128]{2,3,1,0:T(8,128)S(1)} custom-call(f32[1,2,128,128]{3,2,1,0:T(8,128)S(1)} %bitcast.222), custom_call_target="InvertDiagBlocksLowerTriangular" | custom-call | tf_op jit(solution)/shard_map/triangular_solve/custom-call.0 | solution.py:43
  314.4 1.7 copy.14
  316.1 1.4 fusion.38
  318.3 1.3 fusion.24
  (57 shorter events, 16.0 us)
Async XLA Ops:
  7.2 97.4 %all-gather.3.cloned.1.call-start = ((), (), s32[]{:S(2)}) async-start(), calls=%async_computation.3 | async-start | bytes 10485760 | tf_op jit(solution)/shard_map/all_gather | solution.py:24
  14.2 1.2 copy-start.1
  14.2 227.8 %all-reduce.4.cloned.1.call-start = ((), (), s32[]{:S(2)}) async-start(), calls=%async_computation.1 | async-start | bytes 524288 | tf_op jit(solution)/shard_map/psum | solution.py:40
  179.3 4.3 %copy-start.2 = (f32[1,2,128,128]{2,3,1,0:T(8,128)}, f32[1,2,128,128]{2,3,1,0:T(8,128)S(1)}, u32[]{:S(2)}) copy-start(f32[1,2,128,128]{2,3,1,0:T(8,128)S(1)} %custom-call.24) | copy-start | bytes 393220
  186.9 129.1 %reduce-scatter.2.cloned.1.call-start = ((), (), s32[]{:S(2)}) async-start(), calls=%async_computation.2 | async-start | bytes 2621440 | tf_op jit(solution)/shard_map/reduce_scatter | solution.py:41
  314.4 1.7 copy-start.3
  316.1 4.4 %copy-start = (f32[1,256,512]{2,1,0:T(8,128)S(1)}, f32[1,256,512]{2,1,0:T(8,128)}, u32[]{:S(2)}) copy-start(f32[1,256,512]{2,1,0:T(8,128)} %reduce-scatter.2.cloned.1.call-done) | copy-start | bytes 1572868
Sparse Core Ops, SparseCore 0:
  14.3 90.1 all-gather.2
  187.0 43.0 all-reduce.3
  233.1 35.3 reduce-scatter.1
